TPU v7x, 32 devices: a whole 2x2x4 slice. The times are simulated.
32 devices in a mesh: seq: 8 (over z, y), tensor: 4 (over x, core).
Axes of the slice: x: 2, y: 2, z: 4, core: 2. Of those that a mesh axis runs over, the one named last changes fastest.
Arguments:
- hidden_in: bfloat16 [1024, 8192], P('seq', 'tensor'), may hold values from -6 to 6
- grad_out: bfloat16 [1024, 8192], P('seq', 'tensor'), may hold values from -6 to 6
- slot_tokens: int32 [128], P('seq'), may hold values from 0 to 127, as said below
- live_counts: int32 [8], P('seq'), may hold values from 5 to 16, as said below
- norm_gain: float32 [8192], P('tensor'), may hold values from 0.5 to 1.5
- router_weight: float32 [8192], P('tensor'), may hold values from -0.0625 to 0.0625
- gate_weight: bfloat16 [8192, 24576], P('tensor', 'seq'), may hold values from -0.0625 to 0.0625
- up_weight: bfloat16 [8192, 24576], P('tensor', 'seq'), may hold values from -0.0625 to 0.0625
- down_weight: bfloat16 [24576, 8192], P('seq', 'tensor'), may hold values from -0.0390625 to 0.0390625
Outputs:
- grad_in: bfloat16 [1024, 8192], P('seq', 'tensor')
- grad_gate: bfloat16 [8192, 24576], P('tensor', 'seq')
- grad_up: bfloat16 [8192, 24576], P('tensor', 'seq')
- grad_down: bfloat16 [24576, 8192], P('seq', 'tensor')
- grad_gain: float32 [8192], P('tensor')
- grad_router: float32 [8192], P('tensor')
Inputs may be any that keep to these rules, and one draw needn't show every extreme that they name: `slot_tokens`: slot p belongs to index p // 16 of seq; the live slots of one index hold distinct positions, the others hold arbitrary positions of that index. `live_counts`: in every draw some index of seq has all 16 slots live.
All inputs are finite; a program needn't handle non-finite values.
Results may differ from a plain program's by a relative error of at most 0.0077.
Values may be sent and summed in bfloat16 or wider, within the bound.
A program may use at most 128 MiB of HBM per device.

v0:
```python
import functools

import jax
import jax.numpy as jnp
from jax import lax
from jax.experimental import pallas as pl
from jax.experimental.pallas import tpu as pltpu
from jax.sharding import PartitionSpec as P

norm_eps = 1e-06
f32 = jnp.float32
bf16 = jnp.bfloat16
MESH = pl.DeviceIdType.MESH


def pick_chunks(size, options, unit=128):
    for n in options:
        if size % (n * unit) == 0:
            return n
    return 1


def nt_dot(a, b):
    return lax.dot_general(a, b, (((1,), (1,)), ((), ())), preferred_element_type=f32)


def tn_dot(a, b):
    return lax.dot_general(a, b, (((0,), (0,)), ((), ())), preferred_element_type=f32)


def outer_kernel(norm, dg, du, wt, ups, cs, o_gate, o_up, o_down):
    scale = cs[0:1, 0:1]

    def fill(out, left, right):
        size = right.shape[1]
        piece = size // pick_chunks(size, (6, 4, 3, 2))
        for n in range(0, size, piece):
            out[:, n : n + piece] = (tn_dot(left, right[:, n : n + piece]) * scale).astype(bf16)

    fill(o_gate, norm[...], dg)
    fill(o_up, norm[...], du)
    fill(o_down, wt[...], ups)


def outer_products(normed, d_gate, d_up, weighted, upstream, scale):
    rows, width = normed.shape
    hidden = d_gate.shape[1]
    steps = next(n for n in (8, 4, 2, 1) if width % (n * 128) == 0 and hidden % (n * 128) == 0)
    tw, th = width // steps, hidden // steps

    def whole(shape):
        return pl.BlockSpec(shape, lambda i: (0, 0))

    return pl.pallas_call(
        outer_kernel,
        grid=(steps,),
        out_shape=[
            jax.ShapeDtypeStruct((width, hidden), bf16),
            jax.ShapeDtypeStruct((width, hidden), bf16),
            jax.ShapeDtypeStruct((hidden, width), bf16),
        ],
        in_specs=[
            pl.BlockSpec((rows, tw), lambda i: (0, i)),
            whole((rows, hidden)),
            whole((rows, hidden)),
            pl.BlockSpec((rows, th), lambda i: (0, i)),
            whole((rows, width)),
            whole((1, 128)),
        ],
        out_specs=[
            pl.BlockSpec((tw, hidden), lambda i: (i, 0)),
            pl.BlockSpec((tw, hidden), lambda i: (i, 0)),
            pl.BlockSpec((th, width), lambda i: (i, 0)),
        ],
        compiler_params=pltpu.CompilerParams(
            dimension_semantics=("arbitrary",), vmem_limit_bytes=67_043_328
        ),
    )(normed, d_gate, d_up, weighted, upstream, scale)


def kernel(
    ns,
    nt,
    nc,
    nk,
    hid,
    gout,
    tok_col,
    tok_row,
    live,
    gain,
    router,
    wg_hbm,
    wu_hbm,
    wd_hbm,
    o_in,
    o_gr,
    o_w,
    o_dg,
    o_du,
    o_norm,
    o_ups,
    o_cs,
    wg,
    wu,
    wd,
    gath,
    colbuf,
    invbuf,
    logbuf,
    rgbuf,
    rgacc,
    smsg,
    srec,
    imsg,
    irec,
    part,
    drec,
    xsnd,
    xrec,
    acc,
    ysnd,
    yrec,
    zsnd,
    zrec,
    gmsg,
    grec,
    w_sem,
    agz_s,
    agz_r,
    agy_s,
    agy_r,
    sm_s,
    sm_r,
    in_s,
    in_r,
    d_s,
    d_r,
    x_s,
    x_r,
    a_s,
    a_r,
    rg_s,
    rg_r,
    y_s,
    y_r,
    z_s,
    z_r,
    g_s,
    g_r,
):
    tokens, width = hid.shape
    cap = tok_col.shape[0]
    rows = ns * cap
    half = rows // 2
    hidden = wg.shape[1]
    fc = hidden // nc
    kc = width // nk
    nz, nx = ns // 2, nt // 2
    s, t = lax.axis_index("seq"), lax.axis_index("tensor")
    y, z = lax.rem(s, 2), lax.div(s, 2)
    core, x = lax.rem(t, 2), lax.div(t, 2)
    mate = t + 1 - 2 * core
    yp = s + 1 - 2 * y
    mine = pl.multiple_of(core * half, half)

    def remote(src, dst, ssem, rsem, **where):
        return pltpu.make_async_remote_copy(
            src_ref=src,
            dst_ref=dst,
            send_sem=ssem,
            recv_sem=rsem,
            device_id=where,
            device_id_type=MESH,
        )

    loads = [
        pltpu.make_async_copy(wd_hbm, wd, w_sem.at[0]),
        pltpu.make_async_copy(wg_hbm, wg, w_sem.at[1]),
        pltpu.make_async_copy(wu_hbm, wu, w_sem.at[2]),
    ]
    for load in loads:
        load.start()

    barrier = pltpu.get_barrier_semaphore()
    for j in range(1, ns):
        pl.semaphore_signal(
            barrier, inc=1, device_id={"seq": lax.rem(s + j, ns)}, device_id_type=MESH
        )
    for j in range(1, nt):
        pl.semaphore_signal(
            barrier, inc=1, device_id={"tensor": lax.rem(t + j, nt)}, device_id_type=MESH
        )

    hot = (tok_col[...] == lax.broadcasted_iota(jnp.int32, (cap, tokens), 1)).astype(f32)
    live_col = (lax.broadcasted_iota(jnp.int32, (cap, 1), 0) < live[...]).astype(f32)
    gath[s, :, pl.ds(0, width)] = jnp.dot(
        hot.astype(bf16), hid[...], preferred_element_type=f32
    ).astype(bf16)
    gath[s, :, pl.ds(width, width)] = jnp.dot(
        (hot * live_col).astype(bf16), gout[...], preferred_element_type=f32
    ).astype(bf16)
    gath[s, :, pl.ds(2 * width, 128)] = jnp.broadcast_to(
        live[...].astype(f32), (cap, 128)
    ).astype(bf16)
    pl.semaphore_wait(barrier, ns - 1 + nt - 1)

    def agz(j):
        own = gath.at[s]
        return remote(own, own, agz_s.at[j], agz_r.at[j], seq=2 * lax.rem(z + j, nz) + y)

    def agy(j):
        block = gath.at[2 * lax.rem(z + nz - j, nz) + y]
        return remote(block, block, agy_s.at[j], agy_r.at[j], seq=yp)

    def consume(b):
        rows_b = pl.ds(pl.multiple_of(b * cap, cap), cap)
        wide = gath[b, :, pl.ds(0, width)].astype(f32)
        o_ups[rows_b, :] = gath[b, :, pl.ds(width, width)]
        colbuf[rows_b, :] = jnp.broadcast_to(
            jnp.sum(wide * wide, axis=1, keepdims=True), (cap, 128)
        )

    agy(0).start()
    for j in range(1, nz):
        agz(j).start()
    consume(s)

    @pl.loop(1, nz)
    def _(j):
        agz(j).wait_recv()
        agy(j).start()
        consume(2 * lax.rem(z + nz - j, nz) + y)

    @pl.loop(0, nz)
    def _(j):
        agy(j).wait_recv()
        consume(2 * lax.rem(z + nz - j, nz) + 1 - y)

    def small(k, j):
        return remote(
            smsg.at[k], srec.at[k, j], sm_s.at[k, j], sm_r.at[k, j], tensor=lax.rem(t + j, nt)
        )

    def small_send(k):
        smsg[k] = colbuf[...].T[0:8, :]
        for j in range(1, nt):
            small(k, j).start()

    def small_sum(k):
        total = smsg[k]
        for j in range(1, nt):
            small(k, j).wait_recv()
            total = total + srec[k, j]
        return jnp.broadcast_to(total[0:1, :], (128, rows)).T

    small_send(0)

    def pair(a, c):
        return remote(
            part.at[a, c, 1 - core], drec.at[a, c], d_s.at[a, c], d_r.at[a, c], tensor=mate
        )

    def cross(j, a, c):
        return remote(
            xsnd.at[a, c],
            xrec.at[j, a, c],
            x_s.at[j, a, c],
            x_r.at[j, a, c],
            tensor=2 * lax.rem(x + j, nx) + core,
        )

    def emit(a, c, value):
        part[a, c] = value.reshape(2, half, fc)
        pair(a, c).start()

    def relay(a, c):
        pair(a, c).wait_recv()
        total = part[a, c, core] + drec[a, c]
        part[a, c, core] = total
        xsnd[a, c] = total.astype(bf16)
        for j in range(1, nx):
            cross(j, a, c).start()

    def cols(c):
        return pl.ds(pl.multiple_of(c * fc, fc), fc)

    loads[0].wait()

    @pl.loop(0, nc)
    def _(c):
        emit(0, c, nt_dot(o_ups[...], wd[cols(c), :]))

        @pl.when(c > 0)
        def _():
            relay(0, c - 1)

    relay(0, nc - 1)

    width_total = width * nt
    invbuf[...] = lax.rsqrt(small_sum(0) / width_total + norm_eps)
    router_row = router[...].astype(bf16).astype(f32)

    @pl.loop(0, ns)
    def _(b):
        rows_b = pl.ds(pl.multiple_of(b * cap, cap), cap)
        scaled = gath[b, :, pl.ds(0, width)].astype(f32) * invbuf[rows_b, 0:1]
        normed = (scaled * gain[...]).astype(bf16)
        o_norm[rows_b, :] = normed
        colbuf[rows_b, :] = jnp.broadcast_to(
            jnp.sum(normed.astype(f32) * router_row, axis=1, keepdims=True), (cap, 128)
        )

    small_send(1)
    loads[1].wait()
    loads[2].wait()

    @pl.loop(0, nc)
    def _(c):
        emit(1, c, jnp.dot(o_norm[...], wg[:, cols(c)], preferred_element_type=f32))

        @pl.when(c > 0)
        def _():
            relay(2, c - 1)

        emit(2, c, jnp.dot(o_norm[...], wu[:, cols(c)], preferred_element_type=f32))
        relay(1, c)

    relay(2, nc - 1)

    logbuf[...] = small_sum(1)
    rgacc[...] = jnp.zeros_like(rgacc)
    acc[...] = jnp.zeros_like(acc)
    acts = (o_w, o_dg, o_du)

    def act_copy(a, c):
        piece = acts[a].at[pl.ds(mine, half), cols(c)]
        return remote(piece, piece, a_s.at[a, c], a_r.at[a, c], tensor=mate)

    def gate_backward(c):
        for a in range(3):
            for j in range(1, nx):
                cross(j, a, c).wait_recv()

        @pl.loop(0, half // 16)
        def _(r):
            sub = pl.ds(pl.multiple_of(r * 16, 16), 16)
            out = pl.ds(pl.multiple_of(mine + r * 16, 16), 16)
            back, gate, upper = [
                functools.reduce(
                    lambda u, v: u + v,
                    [xrec[j, a, c, sub, :].astype(f32) for j in range(1, nx)],
                    part[a, c, core, sub, :],
                )
                for a in range(3)
            ]
            logit = logbuf[out, 0:1]
            sig = jax.nn.sigmoid(gate)
            act = gate * sig
            slope = sig * (1.0 + gate * (1.0 - sig))
            hid_v = act * upper
            o_w[out, cols(c)] = (hid_v * logit).astype(bf16)
            d_hidden = logit * back
            o_dg[out, cols(c)] = (d_hidden * upper * slope).astype(bf16)
            o_du[out, cols(c)] = (d_hidden * act).astype(bf16)
            terms = hid_v * back
            add = terms[:, 0:128]
            for i in range(1, fc // 128):
                add = add + terms[:, i * 128 : (i + 1) * 128]
            rgacc[sub, :] = rgacc[sub, :] + add

        for a in range(3):
            act_copy(a, c).start()

    def kcols(k):
        return pl.ds(pl.multiple_of(k * kc, kc), kc)

    def back_dots(c, k):
        return nt_dot(o_dg[:, cols(c)], wg[kcols(k), cols(c)]) + nt_dot(
            o_du[:, cols(c)], wu[kcols(k), cols(c)]
        )

    def act_wait(c):
        for a in range(3):
            act_copy(a, c).wait_recv()

    @pl.loop(0, nc)
    def _(c):
        gate_backward(c)

        @pl.when(c > 0)
        def _():
            act_wait(c - 1)

            @pl.loop(0, nk)
            def _(k):
                acc[:, :, kcols(k)] = acc[:, :, kcols(k)] + back_dots(c - 1, k).reshape(
                    ns, cap, kc
                )

    rgbuf[core] = jnp.broadcast_to(jnp.sum(rgacc[...], axis=1, keepdims=True), (half, 128))
    rg_copy = remote(rgbuf.at[core], rgbuf.at[core], rg_s, rg_r, tensor=mate)
    rg_copy.start()
    act_wait(nc - 1)
    rg_copy.wait_recv()

    def ycopy(k):
        return remote(ysnd.at[k], yrec.at[k], y_s.at[k], y_r.at[k], seq=yp)

    def zcopy(j, k):
        return remote(
            zsnd.at[j, k],
            zrec.at[j, k],
            z_s.at[j, k],
            z_r.at[j, k],
            seq=2 * lax.rem(z + j, nz) + y,
        )

    def zstage(k):
        ycopy(k).wait_recv()
        for j in range(1, nz):
            zz = lax.rem(z + j, nz)
            zsnd[j, k] = (acc[2 * zz + y, :, kcols(k)] + yrec[k, zz].astype(f32)).astype(bf16)
            zcopy(j, k).start()
        acc[s, :, kcols(k)] = acc[s, :, kcols(k)] + yrec[k, z].astype(f32)

    @pl.loop(0, nk)
    def _(k):
        rg = jnp.concatenate([rgbuf[0], rgbuf[1]], axis=0)[:, 0:1]
        total = back_dots(nc - 1, k) + rg * router[:, kcols(k)]
        acc[:, :, kcols(k)] = acc[:, :, kcols(k)] + total.reshape(ns, cap, kc)
        for zz in range(nz):
            ysnd[k, zz] = acc[2 * zz + 1 - y, :, kcols(k)].astype(bf16)
        ycopy(k).start()

        @pl.when(k > 0)
        def _():
            zstage(k - 1)

    zstage(nk - 1)

    router_part = jnp.zeros((1, width), f32)
    count = jnp.zeros((1, 128), f32)
    rg_all = jnp.concatenate([rgbuf[0], rgbuf[1]], axis=0)
    for b in range(ns):
        block = o_norm[b * cap : (b + 1) * cap, :].astype(f32)
        router_part = router_part + jnp.sum(
            rg_all[b * cap : (b + 1) * cap, 0:1] * block, axis=0, keepdims=True
        )
        count = count + gath[b, 0:1, 2 * width : 2 * width + 128].astype(f32)
    scale = lax.rsqrt(count)
    o_cs[...] = scale
    gmsg[1:2, :] = router_part

    for j in range(1, nz):

        @pl.loop(0, nk)
        def _(k):
            zcopy(j, k).wait_recv()
            acc[s, :, kcols(k)] = acc[s, :, kcols(k)] + zrec[j, k].astype(f32)

    own = pl.ds(pl.multiple_of(s * cap, cap), cap)
    inverse = invbuf[own, 0:1]
    scaled = gath[s, :, pl.ds(0, width)].astype(f32) * inverse
    d_normed = acc[s]
    d_scaled = d_normed * gain[...]
    imsg[...] = jnp.broadcast_to(jnp.sum(d_scaled * scaled, axis=1, keepdims=True), (cap, 128))

    def inner_copy(j):
        return remote(imsg, irec.at[j], in_s.at[j], in_r.at[j], tensor=lax.rem(t + j, nt))

    def gain_copy(j):
        return remote(gmsg, grec.at[j], g_s.at[j], g_r.at[j], seq=lax.rem(s + j, ns))

    for j in range(1, nt):
        inner_copy(j).start()
    gmsg[0:1, :] = jnp.sum(d_normed * scaled, axis=0, keepdims=True)
    for j in range(1, ns):
        gain_copy(j).start()

    inner = imsg[...]
    for j in range(1, nt):
        inner_copy(j).wait_recv()
        inner = inner + irec[j]
    inner = inner[:, 0:1] / width_total
    d_picked = inverse * (d_scaled - scaled * inner) * live_col
    place = (tok_row[...] == lax.broadcasted_iota(jnp.int32, (tokens, cap), 0)).astype(f32)
    added = jnp.dot(place, d_picked, precision=lax.Precision.HIGHEST, preferred_element_type=f32)
    o_in[...] = (gout[...].astype(f32) + added).astype(bf16)

    total = gmsg[...]
    for j in range(1, ns):
        gain_copy(j).wait_recv()
        total = total + grec[j]
    o_gr[...] = total * scale[:, 0:1]

    agy(0).wait_send()
    for j in range(1, nz):
        agz(j).wait_send()
        agy(j).wait_send()
    for j in range(1, nt):
        small(0, j).wait_send()
        small(1, j).wait_send()
        inner_copy(j).wait_send()
    for j in range(1, ns):
        gain_copy(j).wait_send()
    rg_copy.wait_send()

    @pl.loop(0, nc)
    def _(c):
        for a in range(3):
            pair(a, c).wait_send()
            act_copy(a, c).wait_send()
            for j in range(1, nx):
                cross(j, a, c).wait_send()

    @pl.loop(0, nk)
    def _(k):
        ycopy(k).wait_send()
        for j in range(1, nz):
            zcopy(j, k).wait_send()


def body(
    hidden_in,
    grad_out,
    slot_tokens,
    live_counts,
    norm_gain,
    router_weight,
    gate_weight,
    up_weight,
    down_weight,
):
    ns, nt = lax.axis_size("seq"), lax.axis_size("tensor")
    cap = slot_tokens.shape[0]
    tokens, width = hidden_in.shape
    hidden = gate_weight.shape[1]
    rows, nz, nx = ns * cap, ns // 2, nt // 2
    half = rows // 2
    nc = pick_chunks(hidden, (6, 4, 3, 2))
    nk = pick_chunks(width, (4, 2))
    fc, kc = hidden // nc, width // nk
    vmem = pl.BlockSpec(memory_space=pltpu.VMEM)
    hbm = pl.BlockSpec(memory_space=pl.ANY)
    dma = pltpu.SemaphoreType.DMA
    grad_in, small, weighted, d_gate, d_up, normed, upstream, scale = pl.pallas_call(
        functools.partial(kernel, ns, nt, nc, nk),
        out_shape=[
            jax.ShapeDtypeStruct((tokens, width), bf16),
            jax.ShapeDtypeStruct((2, width), f32),
            jax.ShapeDtypeStruct((rows, hidden), bf16),
            jax.ShapeDtypeStruct((rows, hidden), bf16),
            jax.ShapeDtypeStruct((rows, hidden), bf16),
            jax.ShapeDtypeStruct((rows, width), bf16),
            jax.ShapeDtypeStruct((rows, width), bf16),
            jax.ShapeDtypeStruct((1, 128), f32),
        ],
        in_specs=[vmem] * 7 + [hbm] * 3,
        out_specs=[vmem] * 8,
        scratch_shapes=[
            pltpu.VMEM((width, hidden), bf16),
            pltpu.VMEM((width, hidden), bf16),
            pltpu.VMEM((hidden, width), bf16),
            pltpu.VMEM((ns, cap, 2 * width + 128), bf16),
            pltpu.VMEM((rows, 128), f32),
            pltpu.VMEM((rows, 128), f32),
            pltpu.VMEM((rows, 128), f32),
            pltpu.VMEM((2, half, 128), f32),
            pltpu.VMEM((half, 128), f32),
            pltpu.VMEM((2, 8, rows), f32),
            pltpu.VMEM((2, nt, 8, rows), f32),
            pltpu.VMEM((cap, 128), f32),
            pltpu.VMEM((nt, cap, 128), f32),
            pltpu.VMEM((3, nc, 2, half, fc), f32),
            pltpu.VMEM((3, nc, half, fc), f32),
            pltpu.VMEM((3, nc, half, fc), bf16),
            pltpu.VMEM((nx, 3, nc, half, fc), bf16),
            pltpu.VMEM((ns, cap, width), f32),
            pltpu.VMEM((nk, nz, cap, kc), bf16),
            pltpu.VMEM((nk, nz, cap, kc), bf16),
            pltpu.VMEM((nz, nk, cap, kc), bf16),
            pltpu.VMEM((nz, nk, cap, kc), bf16),
            pltpu.VMEM((2, width), f32),
            pltpu.VMEM((ns, 2, width), f32),
            dma((3,)),
            dma((nz,)),
            dma((nz,)),
            dma((nz,)),
            dma((nz,)),
            dma((2, nt)),
            dma((2, nt)),
            dma((nt,)),
            dma((nt,)),
            dma((3, nc)),
            dma((3, nc)),
            dma((nx, 3, nc)),
            dma((nx, 3, nc)),
            dma((3, nc)),
            dma((3, nc)),
            dma,
            dma,
            dma((nk,)),
            dma((nk,)),
            dma((nz, nk)),
            dma((nz, nk)),
            dma((ns,)),
            dma((ns,)),
        ],
        compiler_params=pltpu.CompilerParams(
            collective_id=0, has_side_effects=True, vmem_limit_bytes=67_043_328
        ),
    )(
        hidden_in,
        grad_out,
        slot_tokens.reshape(cap, 1),
        slot_tokens.reshape(1, cap),
        live_counts.reshape(1, 1),
        norm_gain.reshape(1, width),
        router_weight.reshape(1, width),
        gate_weight,
        up_weight,
        down_weight,
    )
    grad_gate, grad_up, grad_down = outer_products(
        normed, d_gate, d_up, weighted, upstream, scale
    )
    return (grad_in, grad_gate, grad_up, grad_down, small[0], small[1])


def solution(mesh):
    in_specs = (
        P("seq", "tensor"),
        P("seq", "tensor"),
        P("seq"),
        P("seq"),
        P("tensor"),
        P("tensor"),
        P("tensor", "seq"),
        P("tensor", "seq"),
        P("seq", "tensor"),
    )
    out_specs = (
        P("seq", "tensor"),
        P("tensor", "seq"),
        P("tensor", "seq"),
        P("seq", "tensor"),
        P("tensor"),
        P("tensor"),
    )
    return jax.shard_map(body, mesh=mesh, in_specs=in_specs, out_specs=out_specs, check_vma=False)
```

profile of v0, /device:TPU:0, one launch (start us, length us, event | category | flops | bytes accessed | tf_op | source)
XLA Modules:
  0.0 101.5 jit_solution(9535495646427675910)
XLA Ops:
  1.3 1.3 %copy.15.tok_col = s32[16,1]{1,0:T(8,128)} copy(s32[16,1]{0,1:T(1,128)} %bitcast.12) | data formatting | bytes 128 | tf_op jit(solution)/shard_map/reshape | solution.py:616
  2.6 81.1 %shard_map.136 = (bf16[128,2048]{1,0:T(8,128)(2,1)}, f32[2,2048]{1,0:T(2,128)}, bf16[128,3072]{1,0:T(8,128)(2,1)}, bf16[128,3072]{1,0:T(8,128)(2,1)}, bf16[128,3...) custom-call(bf16[128,2048]{1,0:T(8,128)(2,1)} %hid.1, ...), custom_call_target="tpu_custom_call" | custom-call | tf_op jit(solution)/shard_map/pallas_call | solution.py:547
  83.7 1.4 %fusion = (f32[1,2048]{1,0:T(1,128)}, f32[1,2048]{1,0:T(1,128)}) fusion(f32[2,2048]{1,0:T(2,128)} %get-tuple-element.27), kind=kLoop, calls=%fused_computation | loop fusion | bytes 32768 | tf_op jit(solution)/shard_map/slice | solution.py:628
  85.1 14.5 %shard_map.137 = (bf16[2048,3072]{1,0:T(8,128)(2,1)}, bf16[2048,3072]{1,0:T(8,128)(2,1)}, bf16[3072,2048]{1,0:T(8,128)(2,1)}) custom-call(bf16[128,2048]{1,0:T(8,128)(2,1)} %get-tuple-element.18.norm, bf16[128,3072]{1,0:T(8,128)(2,1)} %get-tuple-element.19.dg, bf16[128,3072]{1,0:T(8,128)(2,1)} %get-tuple-element.20.du, ...), custom_call_target="tpu_custom_call" | custom-call | tf_op jit(solution)/shard_map/pallas_call | solution.py:54
  99.6 1.9 %copy.18 = bf16[128,2048]{1,0:T(8,128)(2,1)} copy(bf16[128,2048]{1,0:T(8,128)(2,1)} %get-tuple-element.36) | data formatting | bytes 1048576
where the time goes:
time: 102 us; the launch traced here: 101 us
  Pallas kernels  95.6 us (94%)
  local copies, waits for them, and re-layouts  4.62 us (5%)
  between operations  1.29 us (1%)
    pallas_call x1, Pallas kernels, body(): pl.pallas_call(functools.partial(kernel, ns, nt, nc, nk), out_shape=[jax....  81.1 us
    pallas_call x1, Pallas kernels, outer_products(): pl.pallas_call(outer_kernel, grid=(steps,), out_shape=[jax.ShapeDtypeStru...  14.5 us

commit v1 on v0

v1 whole, which is shorter than its diff:
```python
import functools

import jax
import jax.numpy as jnp
from jax import lax
from jax.experimental import pallas as pl
from jax.experimental.pallas import tpu as pltpu
from jax.sharding import PartitionSpec as P

norm_eps = 1e-06
f32 = jnp.float32
bf16 = jnp.bfloat16
MESH = pl.DeviceIdType.MESH


def pick_chunks(size, options, unit=128):
    for n in options:
        if size % (n * unit) == 0:
            return n
    return 1


def nt_dot(a, b):
    return lax.dot_general(a, b, (((1,), (1,)), ((), ())), preferred_element_type=f32)


def tn_dot(a, b):
    return lax.dot_general(a, b, (((0,), (0,)), ((), ())), preferred_element_type=f32)


def outer_kernel(
    norm, dg, du, wt, ups, hid, gout, dn, gain, sums, cs, col, tok, live, o_gate, o_up, o_down, o_in, o_gain, o_router
):
    scale = cs[0:1, 0:1]

    def fill(out, left, right):
        size = right.shape[1]
        piece = size // pick_chunks(size, (6, 4, 3, 2))
        for n in range(0, size, piece):
            out[:, n : n + piece] = (tn_dot(left, right[:, n : n + piece]) * scale).astype(bf16)

    cap = dn.shape[0]
    place = tok[...] == lax.broadcasted_iota(jnp.int32, (hid.shape[0], cap), 0)
    hot = place.astype(f32).astype(bf16)
    alive = (lax.broadcasted_iota(jnp.int32, (cap, 1), 0) < live[...]).astype(f32)
    inverse = col[0][:, 0:1]
    scaled = tn_dot(hot, hid[...]) * inverse
    d_picked = inverse * (dn[...] * gain[...] - scaled * col[1][:, 0:1]) * alive
    high = d_picked.astype(bf16)
    rest = d_picked - high.astype(f32)
    mid = rest.astype(bf16)
    low = (rest - mid.astype(f32)).astype(bf16)
    fill(o_gate, norm[...], dg)
    added = (
        jnp.dot(hot, high, preferred_element_type=f32)
        + jnp.dot(hot, mid, preferred_element_type=f32)
        + jnp.dot(hot, low, preferred_element_type=f32)
    )
    o_in[...] = (gout[...].astype(f32) + added).astype(bf16)
    o_gain[...] = sums[0:1, :] * scale
    o_router[...] = sums[1:2, :] * scale
    fill(o_up, norm[...], du)
    fill(o_down, wt[...], ups)


def outer_products(
    normed, d_gate, d_up, weighted, upstream, hid, gout, d_normed, gain, sums, cs, col, tok, live
):
    rows, width = normed.shape
    hidden = d_gate.shape[1]
    tokens, cap = hid.shape[0], d_normed.shape[0]
    steps = next(n for n in (8, 4, 2, 1) if width % (n * 128) == 0 and hidden % (n * 128) == 0)
    tw, th = width // steps, hidden // steps

    def whole(shape):
        return pl.BlockSpec(shape, lambda i: (0,) * len(shape))

    def across(height, size):
        return pl.BlockSpec((height, size), lambda i: (0, i))

    return pl.pallas_call(
        outer_kernel,
        grid=(steps,),
        out_shape=[
            jax.ShapeDtypeStruct((width, hidden), bf16),
            jax.ShapeDtypeStruct((width, hidden), bf16),
            jax.ShapeDtypeStruct((hidden, width), bf16),
            jax.ShapeDtypeStruct((tokens, width), bf16),
            jax.ShapeDtypeStruct((1, width), f32),
            jax.ShapeDtypeStruct((1, width), f32),
        ],
        in_specs=[
            across(rows, tw),
            whole((rows, hidden)),
            whole((rows, hidden)),
            across(rows, th),
            whole((rows, width)),
            across(tokens, tw),
            across(tokens, tw),
            across(cap, tw),
            across(1, tw),
            across(2, tw),
            whole(cs.shape),
            whole(col.shape),
            whole(tok.shape),
            whole(live.shape),
        ],
        out_specs=[
            pl.BlockSpec((tw, hidden), lambda i: (i, 0)),
            pl.BlockSpec((tw, hidden), lambda i: (i, 0)),
            pl.BlockSpec((th, width), lambda i: (i, 0)),
            across(tokens, tw),
            across(1, tw),
            across(1, tw),
        ],
        compiler_params=pltpu.CompilerParams(
            dimension_semantics=("arbitrary",), vmem_limit_bytes=67_043_328
        ),
    )(normed, d_gate, d_up, weighted, upstream, hid, gout, d_normed, gain, sums, cs, col, tok, live)


def kernel(
    ns,
    nt,
    nc,
    nk,
    hid,
    gout,
    tok,
    live,
    gain,
    router,
    wg_hbm,
    wu_hbm,
    wd_hbm,
    o_w,
    o_dg,
    o_du,
    o_norm,
    o_ups,
    o_gr,
    o_cs,
    o_dn,
    o_col,
    wg,
    wu,
    wd,
    own,
    qmsg,
    qrec,
    pmsg,
    prec,
    logbuf,
    rgbuf,
    rgacc,
    inacc,
    part,
    drec,
    xsnd,
    xrec,
    acc,
    ysnd,
    yrec,
    zsnd,
    zrec,
    gsnd,
    gyrec,
    gzsnd,
    gzrec,
    w_sem,
    agz_s,
    agz_r,
    agy_s,
    agy_r,
    q_s,
    q_r,
    p_s,
    p_r,
    l_s,
    l_r,
    d_s,
    d_r,
    x_s,
    x_r,
    a_s,
    a_r,
    rg_s,
    rg_r,
    y_s,
    y_r,
    z_s,
    z_r,
    gy_s,
    gy_r,
    gz_s,
    gz_r,
):
    tokens, width = hid.shape
    cap = tok.shape[1]
    rows = ns * cap
    half = rows // 2
    quarter = half // 2
    hidden = wg.shape[1]
    fc = hidden // nc
    kc = width // nk
    nz, nx = ns // 2, nt // 2
    s, t = lax.axis_index("seq"), lax.axis_index("tensor")
    y, z = lax.rem(s, 2), lax.div(s, 2)
    core, x = lax.rem(t, 2), lax.div(t, 2)
    mate = t + 1 - 2 * core
    yp = s + 1 - 2 * y
    zhalf = lax.div(z, nz // 2)
    mine = pl.multiple_of(core * half, half)

    def zx(j):
        total = 0
        bit = 1
        while bit < nz:
            b = lax.rem(lax.div(z, bit), 2)
            total = total + bit * (1 - b if j & bit else b)
            bit *= 2
        return total

    def slot_rows(yy, zz):
        return pl.ds(pl.multiple_of((yy * nz + zz) * cap, cap), cap)

    def remote(src, dst, ssem, rsem, **where):
        return pltpu.make_async_remote_copy(
            src_ref=src,
            dst_ref=dst,
            send_sem=ssem,
            recv_sem=rsem,
            device_id=where,
            device_id_type=MESH,
        )

    loads = [
        pltpu.make_async_copy(wd_hbm, wd, w_sem.at[0]),
        pltpu.make_async_copy(wg_hbm, wg, w_sem.at[1]),
        pltpu.make_async_copy(wu_hbm, wu, w_sem.at[2]),
    ]
    for load in loads:
        load.start()

    barrier = pltpu.get_barrier_semaphore()
    for j in range(1, ns):
        pl.semaphore_signal(
            barrier, inc=1, device_id={"seq": lax.rem(s + j, ns)}, device_id_type=MESH
        )
    for j in range(1, nt):
        pl.semaphore_signal(
            barrier, inc=1, device_id={"tensor": lax.rem(t + j, nt)}, device_id_type=MESH
        )

    width_total = width * nt
    place = tok[...] == lax.broadcasted_iota(jnp.int32, (tokens, cap), 0)
    hot = place.astype(f32).astype(bf16)
    alive = (lax.broadcasted_iota(jnp.int32, (cap, 1), 0) < live[...]).astype(f32)
    own_rows = slot_rows(y, z)
    o_ups[own_rows, :] = (tn_dot(hot, gout[...]) * alive).astype(bf16)
    picked = tn_dot(hot, hid[...])
    own[...] = picked
    qmsg[...] = jnp.broadcast_to(jnp.sum(picked * picked, axis=1, keepdims=True), (cap, 128))
    pl.semaphore_wait(barrier, ns - 1 + nt - 1)

    gathered = (o_ups, o_norm)

    def agz(m, j):
        block = gathered[m].at[own_rows]
        return remote(block, block, agz_s.at[m, j], agz_r.at[m, j], seq=2 * zx(j) + y)

    def agy(m, j):
        block = gathered[m].at[slot_rows(y, zx(j))]
        return remote(block, block, agy_s.at[m, j], agy_r.at[m, j], seq=yp)

    def square_copy(j):
        return remote(qmsg, qrec.at[j], q_s.at[j], q_r.at[j], tensor=lax.rem(t + j, nt))

    def spread(m):
        agy(m, 0).start()
        for j in range(1, nz):
            agz(m, j).start()

    def pass_on(m, js):
        for j in js:
            agz(m, j).wait_recv()
            agy(m, j).start()

    def arrived(m, js):
        for j in js:
            agy(m, j).wait_recv()

    for j in range(1, nt):
        square_copy(j).start()
    spread(0)
    total = qmsg[...]
    for j in range(1, nt):
        square_copy(j).wait_recv()
        total = total + qrec[j]
    inverse = lax.rsqrt(total / width_total + norm_eps)
    o_col[0] = inverse
    normed = (own[...] * inverse[:, 0:1] * gain[...]).astype(bf16)
    o_norm[own_rows, :] = normed
    router_row = router[...].astype(bf16).astype(f32)
    pmsg[...] = jnp.broadcast_to(
        jnp.sum(normed.astype(f32) * router_row, axis=1, keepdims=True), (cap, 128)
    )

    def logit_part(j):
        return remote(pmsg, prec.at[j], p_s.at[j], p_r.at[j], tensor=lax.rem(t + j, nt))

    def logit_copy(j):
        piece = logbuf.at[own_rows, :]
        return remote(piece, piece, l_s.at[j], l_r.at[j], seq=lax.rem(s + j, ns))

    def share_logits():
        total = pmsg[...]
        for j in range(1, nt):
            logit_part(j).wait_recv()
            total = total + prec[j]
        logbuf[own_rows, :] = total
        for j in range(1, ns):
            logit_copy(j).start()

    near, far = range(1, nz // 2), range(nz // 2, nz)
    for j in range(1, nt):
        logit_part(j).start()
    pass_on(0, near)
    spread(1)

    def item(i):
        if i < 2:
            h = zhalf if i == 0 else 1 - zhalf
            return 0, pl.ds(pl.multiple_of(h * quarter, quarter), quarter)
        return i - 1, pl.ds(0, half)

    def pair(i, c):
        a, span = item(i)
        return remote(
            part.at[a, c, 1 - core, span],
            drec.at[a, c, span],
            d_s.at[i, c],
            d_r.at[i, c],
            tensor=mate,
        )

    def cross(j, i, c):
        a, span = item(i)
        return remote(
            xsnd.at[a, c, span],
            xrec.at[j, a, c, span],
            x_s.at[j, i, c],
            x_r.at[j, i, c],
            tensor=2 * lax.rem(x + j, nx) + core,
        )

    def emit(i, c, value):
        a, span = item(i)
        value = value.reshape(2, -1, fc)
        part[a, c, 0, span, :] = value[0]
        part[a, c, 1, span, :] = value[1]
        pair(i, c).start()

    def relay(i, c):
        a, span = item(i)
        pair(i, c).wait_recv()
        total = part[a, c, core, span, :] + drec[a, c, span, :]
        part[a, c, core, span, :] = total
        xsnd[a, c, span, :] = total.astype(bf16)
        for j in range(1, nx):
            cross(j, i, c).start()

    def cols(c):
        return pl.ds(pl.multiple_of(c * fc, fc), fc)

    def back_pass(i, start, stop):
        _, span = item(i)
        upper_span = pl.ds(pl.multiple_of(half + span.start, quarter), quarter)

        @pl.loop(start, stop)
        def _(c):
            left = jnp.concatenate([o_ups[span, :], o_ups[upper_span, :]], axis=0)
            emit(i, c, nt_dot(left, wd[cols(c), :]))
            if i == 1 and start == 0:

                @pl.when(c == 0)
                def _():
                    relay(0, nc - 1)

            @pl.when(c > 1)
            def _():
                relay(i, c - 2)

    cut, cut2 = nc // 3, 2 * nc // 3
    loads[0].wait()
    arrived(0, [0, *near])
    back_pass(0, 0, cut)
    share_logits()
    pass_on(0, far)
    back_pass(0, cut, cut2)
    pass_on(1, near)
    back_pass(0, cut2, nc)
    relay(0, nc - 2)
    arrived(0, far)
    back_pass(1, 0, cut)
    pass_on(1, far)
    back_pass(1, cut, nc)
    relay(1, nc - 2)
    arrived(1, range(nz))
    loads[1].wait()
    loads[2].wait()

    @pl.loop(0, nc)
    def _(c):
        emit(2, c, jnp.dot(o_norm[...], wg[:, cols(c)], preferred_element_type=f32))

        @pl.when(c == 0)
        def _():
            relay(1, nc - 1)

        @pl.when(c > 0)
        def _():
            relay(2, c - 1)

        emit(3, c, jnp.dot(o_norm[...], wu[:, cols(c)], preferred_element_type=f32))

        @pl.when(c > 0)
        def _():
            relay(3, c - 1)

    relay(2, nc - 1)
    relay(3, nc - 1)

    for j in range(1, ns):
        logit_copy(j).wait_recv()
    rgacc[...] = jnp.zeros_like(rgacc)
    inacc[...] = jnp.zeros_like(inacc)
    acc[...] = jnp.zeros_like(acc)
    acts = (o_w, o_dg, o_du)

    def act_copy(a, c):
        piece = acts[a].at[pl.ds(mine, half), cols(c)]
        return remote(piece, piece, a_s.at[a, c], a_r.at[a, c], tensor=mate)

    def lanes(terms):
        add = terms[:, 0:128]
        for i in range(1, fc // 128):
            add = add + terms[:, i * 128 : (i + 1) * 128]
        return add

    def gate_backward(c):
        for i in range(4):
            for j in range(1, nx):
                cross(j, i, c).wait_recv()

        @pl.loop(0, half // 16)
        def _(r):
            sub = pl.ds(pl.multiple_of(r * 16, 16), 16)
            out = pl.ds(pl.multiple_of(mine + r * 16, 16), 16)
            back, gate, upper = [
                functools.reduce(
                    lambda u, v: u + v,
                    [xrec[j, a, c, sub, :].astype(f32) for j in range(1, nx)],
                    part[a, c, core, sub, :],
                )
                for a in range(3)
            ]
            logit = logbuf[out, 0:1]
            sig = jax.nn.sigmoid(gate)
            act = gate * sig
            slope = sig * (1.0 + gate * (1.0 - sig))
            hid_v = act * upper
            d_hidden = logit * back
            d_gate = (d_hidden * upper * slope).astype(bf16)
            d_up = (d_hidden * act).astype(bf16)
            o_w[out, cols(c)] = (hid_v * logit).astype(bf16)
            o_dg[out, cols(c)] = d_gate
            o_du[out, cols(c)] = d_up
            rgacc[sub, :] = rgacc[sub, :] + lanes(hid_v * back)
            inacc[sub, :] = inacc[sub, :] + lanes(
                d_gate.astype(f32) * gate + d_up.astype(f32) * upper
            )

        for a in range(3):
            act_copy(a, c).start()

    def kcols(k):
        return pl.ds(pl.multiple_of(k * kc, kc), kc)

    def back_dots(c, k):
        return nt_dot(o_dg[:, cols(c)], wg[kcols(k), cols(c)]) + nt_dot(
            o_du[:, cols(c)], wu[kcols(k), cols(c)]
        )

    def act_wait(c):
        for a in range(3):
            act_copy(a, c).wait_recv()

    na = nk // 2 if nk % 2 == 0 else nk
    ka = width // na

    def accumulate(c):
        act_wait(c)

        @pl.loop(0, na)
        def _(k):
            wide = pl.ds(pl.multiple_of(k * ka, ka), ka)
            total = nt_dot(o_dg[:, cols(c)], wg[wide, cols(c)]) + nt_dot(
                o_du[:, cols(c)], wu[wide, cols(c)]
            )
            acc[:, :, wide] = acc[:, :, wide] + total.reshape(ns, cap, ka)

    @pl.loop(0, nc - 1)
    def _(c):
        gate_backward(c)

        @pl.when(c > 0)
        def _():
            accumulate(c - 1)

    gate_backward(nc - 1)
    rg_half = jnp.sum(rgacc[...], axis=1, keepdims=True)
    in_half = jnp.sum(inacc[...], axis=1, keepdims=True)
    in_half = in_half + rg_half * logbuf[pl.ds(mine, half), 0:1]
    first = lax.broadcasted_iota(jnp.int32, (half, 128), 1) < 64
    rgbuf[pl.ds(mine, half), :] = jnp.where(first, rg_half, in_half)
    rg_piece = rgbuf.at[pl.ds(mine, half), :]
    rg_copy = remote(rg_piece, rg_piece, rg_s, rg_r, tensor=mate)
    rg_copy.start()
    accumulate(nc - 2)
    act_wait(nc - 1)
    rg_copy.wait_recv()

    def ycopy(k):
        return remote(ysnd.at[k], yrec.at[k], y_s.at[k], y_r.at[k], seq=yp)

    def zcopy(j, k):
        return remote(
            zsnd.at[j, k],
            zrec.at[j, k],
            z_s.at[j, k],
            z_r.at[j, k],
            seq=2 * zx(j) + y,
        )

    def zstage(k):
        ycopy(k).wait_recv()
        for j in range(1, nz):
            zz = zx(j)
            zsnd[j, k] = (acc[y * nz + zz, :, kcols(k)] + yrec[k, zz].astype(f32)).astype(bf16)
            zcopy(j, k).start()
        acc[y * nz + z, :, kcols(k)] = acc[y * nz + z, :, kcols(k)] + yrec[k, z].astype(f32)

    def finish(k):
        total = back_dots(nc - 1, k) + rgbuf[:, 0:1] * router[:, kcols(k)]
        total = acc[:, :, kcols(k)] + total.reshape(ns, cap, kc)
        acc[:, :, kcols(k)] = total
        for zz in range(nz):
            ysnd[k, zz] = acc[(1 - y) * nz + zz, :, kcols(k)].astype(bf16)
        gsnd[0:1, kcols(k)] = jnp.sum(
            total.reshape(rows, kc) * o_norm[:, kcols(k)].astype(f32), axis=0, keepdims=True
        ) / gain[:, kcols(k)]

    @pl.loop(0, nk - 1)
    def _(k):
        finish(k)
        ycopy(k).start()

    extra = gsnd.shape[1] - width
    gsnd[0:1, pl.ds(width, extra)] = rgbuf[...].T[64:65, :]
    gsnd[1:2, pl.ds(width, extra)] = jnp.broadcast_to(live[...].astype(f32), (1, extra))
    router_part = jnp.zeros((1, width), f32)
    for b in range(ns):
        block = o_norm[b * cap : (b + 1) * cap, :].astype(f32)
        router_part = router_part + jnp.sum(
            rgbuf[b * cap : (b + 1) * cap, 0:1] * block, axis=0, keepdims=True
        )
    gsnd[1:2, pl.ds(0, width)] = router_part
    finish(nk - 1)
    gy_copy = remote(gsnd, gyrec, gy_s, gy_r, seq=yp)
    gy_copy.start()
    ycopy(nk - 1).start()

    def gz_copy(j):
        return remote(gzsnd, gzrec.at[j], gz_s.at[j], gz_r.at[j], seq=2 * zx(j) + y)

    @pl.loop(0, nk - 1)
    def _(k):
        zstage(k)

    gy_copy.wait_recv()
    gzsnd[...] = gsnd[...] + gyrec[...]
    for j in range(1, nz):
        gz_copy(j).start()
    zstage(nk - 1)

    o_dn[...] = acc[y * nz + z]
    for j in range(1, nz):

        @pl.loop(0, nk)
        def _(k):
            zcopy(j, k).wait_recv()
            o_dn[:, kcols(k)] = o_dn[:, kcols(k)] + zrec[j, k].astype(f32)

    total = gzsnd[...]
    for j in range(1, nz):
        gz_copy(j).wait_recv()
        total = total + gzrec[j]
    o_gr[...] = total[:, 0:width]
    o_cs[...] = lax.rsqrt(total[1:2, width : width + 128])
    here = (y * nz + z) * cap + lax.broadcasted_iota(jnp.int32, (cap, extra), 0)
    pick = here == lax.broadcasted_iota(jnp.int32, (cap, extra), 1)
    inner = jnp.sum(jnp.where(pick, total[0:1, width:], 0.0), axis=1, keepdims=True)
    o_col[1] = jnp.broadcast_to(inner / width_total, (cap, 128))

    for m in range(2):
        agy(m, 0).wait_send()
        for j in range(1, nz):
            agz(m, j).wait_send()
            agy(m, j).wait_send()
    for j in range(1, nt):
        square_copy(j).wait_send()
        logit_part(j).wait_send()
    for j in range(1, ns):
        logit_copy(j).wait_send()
    gy_copy.wait_send()
    for j in range(1, nz):
        gz_copy(j).wait_send()
    rg_copy.wait_send()

    @pl.loop(0, nc)
    def _(c):
        for i in range(4):
            pair(i, c).wait_send()
            for j in range(1, nx):
                cross(j, i, c).wait_send()
        for a in range(3):
            act_copy(a, c).wait_send()

    @pl.loop(0, nk)
    def _(k):
        ycopy(k).wait_send()
        for j in range(1, nz):
            zcopy(j, k).wait_send()


def body(
    hidden_in,
    grad_out,
    slot_tokens,
    live_counts,
    norm_gain,
    router_weight,
    gate_weight,
    up_weight,
    down_weight,
):
    ns, nt = lax.axis_size("seq"), lax.axis_size("tensor")
    cap = slot_tokens.shape[0]
    tokens, width = hidden_in.shape
    hidden = gate_weight.shape[1]
    rows, nz, nx = ns * cap, ns // 2, nt // 2
    half = rows // 2
    nc = pick_chunks(hidden, (6, 4, 3, 2))
    nk = pick_chunks(width, (4, 2))
    fc, kc = hidden // nc, width // nk
    wide = width + rows
    vmem = pl.BlockSpec(memory_space=pltpu.VMEM)
    hbm = pl.BlockSpec(memory_space=pl.ANY)
    dma = pltpu.SemaphoreType.DMA
    tok = slot_tokens.reshape(1, cap)
    live = live_counts.reshape(1, 1)
    gain = norm_gain.reshape(1, width)
    weighted, d_gate, d_up, normed, upstream, sums, scale, d_normed, column = pl.pallas_call(
        functools.partial(kernel, ns, nt, nc, nk),
        out_shape=[
            jax.ShapeDtypeStruct((rows, hidden), bf16),
            jax.ShapeDtypeStruct((rows, hidden), bf16),
            jax.ShapeDtypeStruct((rows, hidden), bf16),
            jax.ShapeDtypeStruct((rows, width), bf16),
            jax.ShapeDtypeStruct((rows, width), bf16),
            jax.ShapeDtypeStruct((2, width), f32),
            jax.ShapeDtypeStruct((1, 128), f32),
            jax.ShapeDtypeStruct((cap, width), f32),
            jax.ShapeDtypeStruct((2, cap, 128), f32),
        ],
        in_specs=[vmem] * 6 + [hbm] * 3,
        out_specs=[vmem] * 9,
        scratch_shapes=[
            pltpu.VMEM((width, hidden), bf16),
            pltpu.VMEM((width, hidden), bf16),
            pltpu.VMEM((hidden, width), bf16),
            pltpu.VMEM((cap, width), f32),
            pltpu.VMEM((cap, 128), f32),
            pltpu.VMEM((nt, cap, 128), f32),
            pltpu.VMEM((cap, 128), f32),
            pltpu.VMEM((nt, cap, 128), f32),
            pltpu.VMEM((rows, 128), f32),
            pltpu.VMEM((rows, 128), f32),
            pltpu.VMEM((half, 128), f32),
            pltpu.VMEM((half, 128), f32),
            pltpu.VMEM((3, nc, 2, half, fc), f32),
            pltpu.VMEM((3, nc, half, fc), f32),
            pltpu.VMEM((3, nc, half, fc), bf16),
            pltpu.VMEM((nx, 3, nc, half, fc), bf16),
            pltpu.VMEM((ns, cap, width), f32),
            pltpu.VMEM((nk, nz, cap, kc), bf16),
            pltpu.VMEM((nk, nz, cap, kc), bf16),
            pltpu.VMEM((nz, nk, cap, kc), bf16),
            pltpu.VMEM((nz, nk, cap, kc), bf16),
            pltpu.VMEM((2, wide), f32),
            pltpu.VMEM((2, wide), f32),
            pltpu.VMEM((2, wide), f32),
            pltpu.VMEM((nz, 2, wide), f32),
            dma((3,)),
            dma((2, nz)),
            dma((2, nz)),
            dma((2, nz)),
            dma((2, nz)),
            dma((nt,)),
            dma((nt,)),
            dma((nt,)),
            dma((nt,)),
            dma((ns,)),
            dma((ns,)),
            dma((4, nc)),
            dma((4, nc)),
            dma((nx, 4, nc)),
            dma((nx, 4, nc)),
            dma((3, nc)),
            dma((3, nc)),
            dma,
            dma,
            dma((nk,)),
            dma((nk,)),
            dma((nz, nk)),
            dma((nz, nk)),
            dma,
            dma,
            dma((nz,)),
            dma((nz,)),
        ],
        compiler_params=pltpu.CompilerParams(
            collective_id=0, has_side_effects=True, vmem_limit_bytes=67_043_328
        ),
    )(
        hidden_in,
        grad_out,
        tok,
        live,
        gain,
        router_weight.reshape(1, width),
        gate_weight,
        up_weight,
        down_weight,
    )
    grad_gate, grad_up, grad_down, grad_in, grad_gain, grad_router = outer_products(
        normed,
        d_gate,
        d_up,
        weighted,
        upstream,
        hidden_in,
        grad_out,
        d_normed,
        gain,
        sums,
        scale,
        column,
        tok,
        live,
    )
    return (
        grad_in,
        grad_gate,
        grad_up,
        grad_down,
        grad_gain.reshape(width),
        grad_router.reshape(width),
    )


def solution(mesh):
    in_specs = (
        P("seq", "tensor"),
        P("seq", "tensor"),
        P("seq"),
        P("seq"),
        P("tensor"),
        P("tensor"),
        P("tensor", "seq"),
        P("tensor", "seq"),
        P("seq", "tensor"),
    )
    out_specs = (
        P("seq", "tensor"),
        P("tensor", "seq"),
        P("tensor", "seq"),
        P("seq", "tensor"),
        P("tensor"),
        P("tensor"),
    )
    return jax.shard_map(body, mesh=mesh, in_specs=in_specs, out_specs=out_specs, check_vma=False)
```

time: 102 us -> 84.3 us (0.83)
  Pallas kernels: 95.6 us -> 82.8 us
  local copies, waits for them, and re-layouts: 4.62 us -> 0 us
    pallas_call x1, Pallas kernels: 81.1 us -> 66.5 us  [body(): pl.pallas_call(functools.partial(kernel, ns, nt, nc, nk), out_shape=[jax....]
    unnamed x1 -> x0, local copies, waits for them, and re-layouts: 1.88 us -> none
    pallas_call x1, Pallas kernels: 14.5 us -> 16.3 us  [outer_products(): pl.pallas_call(outer_kernel, grid=(steps,), out_shape=[jax.ShapeDtypeStru...]
    slice x1 -> x0, local copies, waits for them, and re-layouts: 1.41 us -> none  [body(): return (grad_in, grad_gate, grad_up, grad_down, small[0], small[1])]
    reshape x1 -> x0, local copies, waits for them, and re-layouts: 1.33 us -> none  [body(): slot_tokens.reshape(cap, 1)]
where the time goes in v1:
time: 84.3 us; the launch traced here: 84.1 us
  Pallas kernels  82.8 us (98%)
  between operations  1.29 us (2%)
    pallas_call x1, Pallas kernels, body(): pl.pallas_call(functools.partial(kernel, ns, nt, nc, nk), out_shape=[jax....  66.5 us
    pallas_call x1, Pallas kernels, outer_products(): pl.pallas_call(outer_kernel, grid=(steps,), out_shape=[jax.ShapeDtypeStru...  16.3 us

profile of v1, /device:TPU:0, one launch (start us, length us, event | category | flops | bytes accessed | tf_op | source)
XLA Modules:
  0.0 84.1 jit_solution(2675428832571039773)
XLA Ops:
  1.3 66.5 %shard_map.136 = (bf16[128,3072]{1,0:T(8,128)(2,1)}, bf16[128,3072]{1,0:T(8,128)(2,1)}, bf16[128,3072]{1,0:T(8,128)(2,1)}, bf16[128,2048]{1,0:T(8,128)(2,1)}, bf...) custom-call(bf16[128,2048]{1,0:T(8,128)(2,1)} %hid.3, ...), custom_call_target="tpu_custom_call" | custom-call | tf_op jit(solution)/shard_map/pallas_call | solution.py:674
  67.8 16.3 %shard_map.137 = (bf16[2048,3072]{1,0:T(8,128)(2,1)}, bf16[2048,3072]{1,0:T(8,128)(2,1)}, bf16[3072,2048]{1,0:T(8,128)(2,1)}, bf16[128,2048]{1,0:T(8,128)(2,1)}, f32[1,2048]{1,0:T(1,128)}, /*index=5*/f32[1,2048]{1,0:T(1,128)}) custom-call(bf16[128,2048]{1,0:T(8,128)(2,1)} %get-tuple-element.21.norm, bf16[128,3072]{1,0:T(8,128)(2,1)} %get-tuple-element.22.dg, ...), custom_call_target="tpu_custom_call" | custom-call | tf_op jit(solution)/shard_map/pallas_call | solution.py:81

commit v2 on v1

--- a/solution.py
+++ b/solution.py
@@ -29,9 +29,41 @@
 
 
 def outer_kernel(
-    norm, dg, du, wt, ups, hid, gout, dn, gain, sums, cs, col, tok, live, o_gate, o_up, o_down, o_in, o_gain, o_router
+    norm, dg, du, wt, ups, cs, tok, gout_hbm, fin_hbm, o_gate, o_up, o_down, o_in, o_gain, o_router, gout, fin, sem
 ):
     scale = cs[0:1, 0:1]
+    step = pl.program_id(0)
+    tokens = o_in.shape[0]
+    cap = tok.shape[1]
+    loads = [
+        pltpu.make_async_copy(gout_hbm, gout, sem.at[0]),
+        pltpu.make_async_copy(fin_hbm, fin, sem.at[1]),
+    ]
+
+    @pl.when(step == 0)
+    def _():
+        for load in loads:
+            load.start()
+
+    @pl.when(step == pl.num_programs(0) // 2)
+    def _():
+        for load in loads:
+            load.wait()
+        o_gain[...] = fin[cap : cap + 1, :]
+        o_router[...] = fin[cap + 1 : cap + 2, :]
+        place = tok[...] == lax.broadcasted_iota(jnp.int32, (tokens, cap), 0)
+        hot = place.astype(f32).astype(bf16)
+        d_picked = fin[0:cap, :]
+        high = d_picked.astype(bf16)
+        rest = d_picked - high.astype(f32)
+        mid = rest.astype(bf16)
+        low = (rest - mid.astype(f32)).astype(bf16)
+        added = jnp.dot(
+            jnp.concatenate([hot, hot, hot], axis=1),
+            jnp.concatenate([high, mid, low], axis=0),
+            preferred_element_type=f32,
+        )
+        o_in[...] = (gout[...].astype(f32) + added).astype(bf16)
 
     def fill(out, left, right):
         size = right.shape[1]
@@ -39,44 +71,20 @@
         for n in range(0, size, piece):
             out[:, n : n + piece] = (tn_dot(left, right[:, n : n + piece]) * scale).astype(bf16)
 
-    cap = dn.shape[0]
-    place = tok[...] == lax.broadcasted_iota(jnp.int32, (hid.shape[0], cap), 0)
-    hot = place.astype(f32).astype(bf16)
-    alive = (lax.broadcasted_iota(jnp.int32, (cap, 1), 0) < live[...]).astype(f32)
-    inverse = col[0][:, 0:1]
-    scaled = tn_dot(hot, hid[...]) * inverse
-    d_picked = inverse * (dn[...] * gain[...] - scaled * col[1][:, 0:1]) * alive
-    high = d_picked.astype(bf16)
-    rest = d_picked - high.astype(f32)
-    mid = rest.astype(bf16)
-    low = (rest - mid.astype(f32)).astype(bf16)
     fill(o_gate, norm[...], dg)
-    added = (
-        jnp.dot(hot, high, preferred_element_type=f32)
-        + jnp.dot(hot, mid, preferred_element_type=f32)
-        + jnp.dot(hot, low, preferred_element_type=f32)
-    )
-    o_in[...] = (gout[...].astype(f32) + added).astype(bf16)
-    o_gain[...] = sums[0:1, :] * scale
-    o_router[...] = sums[1:2, :] * scale
     fill(o_up, norm[...], du)
     fill(o_down, wt[...], ups)
 
 
-def outer_products(
-    normed, d_gate, d_up, weighted, upstream, hid, gout, d_normed, gain, sums, cs, col, tok, live
-):
+def outer_products(normed, d_gate, d_up, weighted, upstream, cs, tok, gout, fin):
     rows, width = normed.shape
     hidden = d_gate.shape[1]
-    tokens, cap = hid.shape[0], d_normed.shape[0]
+    tokens = gout.shape[0]
     steps = next(n for n in (8, 4, 2, 1) if width % (n * 128) == 0 and hidden % (n * 128) == 0)
     tw, th = width // steps, hidden // steps
 
     def whole(shape):
-        return pl.BlockSpec(shape, lambda i: (0,) * len(shape))
-
-    def across(height, size):
-        return pl.BlockSpec((height, size), lambda i: (0, i))
+        return pl.BlockSpec(shape, lambda i: (0, 0))
 
     return pl.pallas_call(
         outer_kernel,
@@ -90,33 +98,33 @@
             jax.ShapeDtypeStruct((1, width), f32),
         ],
         in_specs=[
-            across(rows, tw),
+            pl.BlockSpec((rows, tw), lambda i: (0, i)),
             whole((rows, hidden)),
             whole((rows, hidden)),
-            across(rows, th),
+            pl.BlockSpec((rows, th), lambda i: (0, i)),
             whole((rows, width)),
-            across(tokens, tw),
-            across(tokens, tw),
-            across(cap, tw),
-            across(1, tw),
-            across(2, tw),
             whole(cs.shape),
-            whole(col.shape),
             whole(tok.shape),
-            whole(live.shape),
+            pl.BlockSpec(memory_space=pl.ANY),
+            pl.BlockSpec(memory_space=pl.ANY),
         ],
         out_specs=[
             pl.BlockSpec((tw, hidden), lambda i: (i, 0)),
             pl.BlockSpec((tw, hidden), lambda i: (i, 0)),
             pl.BlockSpec((th, width), lambda i: (i, 0)),
-            across(tokens, tw),
-            across(1, tw),
-            across(1, tw),
+            whole((tokens, width)),
+            whole((1, width)),
+            whole((1, width)),
+        ],
+        scratch_shapes=[
+            pltpu.VMEM(gout.shape, bf16),
+            pltpu.VMEM(fin.shape, f32),
+            pltpu.SemaphoreType.DMA((2,)),
         ],
         compiler_params=pltpu.CompilerParams(
             dimension_semantics=("arbitrary",), vmem_limit_bytes=67_043_328
         ),
-    )(normed, d_gate, d_up, weighted, upstream, hid, gout, d_normed, gain, sums, cs, col, tok, live)
+    )(normed, d_gate, d_up, weighted, upstream, cs, tok, gout, fin)
 
 
 def kernel(
@@ -133,19 +141,25 @@
     wg_hbm,
     wu_hbm,
     wd_hbm,
+    h_w,
+    h_dg,
+    h_du,
+    h_norm,
+    h_ups,
+    h_cs,
+    h_fin,
     o_w,
     o_dg,
     o_du,
     o_norm,
     o_ups,
-    o_gr,
     o_cs,
-    o_dn,
-    o_col,
+    o_fin,
     wg,
     wu,
     wd,
     own,
+    invbuf,
     qmsg,
     qrec,
     pmsg,
@@ -163,15 +177,22 @@
     yrec,
     zsnd,
     zrec,
-    gsnd,
-    gyrec,
-    gzsnd,
-    gzrec,
+    asnd,
+    ayrec,
+    azsnd,
+    azrec,
+    bsnd,
+    byrec,
+    bzsnd,
+    bzrec,
     w_sem,
+    h_sem,
     agz_s,
     agz_r,
     agy_s,
     agy_r,
+    agd_s,
+    agd_r,
     q_s,
     q_r,
     p_s,
@@ -241,6 +262,15 @@
     ]
     for load in loads:
         load.start()
+    results = [
+        pltpu.make_async_copy(o_w, h_w, h_sem.at[0]),
+        pltpu.make_async_copy(o_dg, h_dg, h_sem.at[1]),
+        pltpu.make_async_copy(o_du, h_du, h_sem.at[2]),
+        pltpu.make_async_copy(o_norm, h_norm, h_sem.at[3]),
+        pltpu.make_async_copy(o_ups, h_ups, h_sem.at[4]),
+        pltpu.make_async_copy(o_cs, h_cs, h_sem.at[5]),
+        pltpu.make_async_copy(o_fin, h_fin, h_sem.at[6]),
+    ]
 
     barrier = pltpu.get_barrier_semaphore()
     for j in range(1, ns):
@@ -269,36 +299,76 @@
         block = gathered[m].at[own_rows]
         return remote(block, block, agz_s.at[m, j], agz_r.at[m, j], seq=2 * zx(j) + y)
 
-    def agy(m, j):
-        block = gathered[m].at[slot_rows(y, zx(j))]
-        return remote(block, block, agy_s.at[m, j], agy_r.at[m, j], seq=yp)
+    near, far = range(1, nz // 2), range(nz // 2)
+    nzh = nz // 2
+    rank = (1 - zhalf) * (nzh - 1 - z) + zhalf * (z - nzh)
+
+    def far_z(f):
+        return zhalf * (nzh - 1 - f) + (1 - zhalf) * (nzh + f)
+
+    def agf(m, f):
+        block = gathered[m].at[own_rows]
+        return remote(
+            block, block, agz_s.at[m, nzh + f], agz_r.at[m, nzh + rank], seq=2 * far_z(f) + y
+        )
+
+    def agf_in(m, f):
+        block = gathered[m].at[slot_rows(y, far_z(f))]
+        return remote(
+            block, block, agz_s.at[m, nzh + f], agz_r.at[m, nzh + f], seq=2 * far_z(f) + y
+        )
+
+    def agy_own(m):
+        block = gathered[m].at[own_rows]
+        return remote(block, block, agy_s.at[m, 0], agy_r.at[m, 0], seq=yp)
+
+    def agy(m, f):
+        block = gathered[m].at[slot_rows(y, far_z(f))]
+        return remote(block, block, agy_s.at[m, nzh + f], agy_r.at[m, nzh + f], seq=yp)
+
+    def agd(m, j):
+        block = gathered[m].at[own_rows]
+        return remote(block, block, agd_s.at[m, j], agd_r.at[m, j], seq=2 * zx(j) + 1 - y)
 
     def square_copy(j):
         return remote(qmsg, qrec.at[j], q_s.at[j], q_r.at[j], tensor=lax.rem(t + j, nt))
 
-    def spread(m):
-        agy(m, 0).start()
-        for j in range(1, nz):
+    def spread_near(m):
+        agy_own(m).start()
+        for j in near:
             agz(m, j).start()
-
-    def pass_on(m, js):
-        for j in js:
+            agd(m, j).start()
+
+    def spread_far(m, fs):
+        for f in fs:
+            agf(m, f).start()
+
+    def pass_on(m, fs):
+        for f in fs:
+            agf_in(m, f).wait_recv()
+            agy(m, f).start()
+
+    def arrived_near(m):
+        agy_own(m).wait_recv()
+        for j in near:
             agz(m, j).wait_recv()
-            agy(m, j).start()
-
-    def arrived(m, js):
-        for j in js:
+            agd(m, j).wait_recv()
+
+    def arrived_far(m):
+        for j in far:
             agy(m, j).wait_recv()
 
     for j in range(1, nt):
         square_copy(j).start()
-    spread(0)
+    spread_near(0)
+    spread_far(0, far[:1])
     total = qmsg[...]
     for j in range(1, nt):
         square_copy(j).wait_recv()
         total = total + qrec[j]
+    spread_far(0, far[1:])
     inverse = lax.rsqrt(total / width_total + norm_eps)
-    o_col[0] = inverse
+    invbuf[...] = inverse
     normed = (own[...] * inverse[:, 0:1] * gain[...]).astype(bf16)
     o_norm[own_rows, :] = normed
     router_row = router[...].astype(bf16).astype(f32)
@@ -322,17 +392,16 @@
         for j in range(1, ns):
             logit_copy(j).start()
 
-    near, far = range(1, nz // 2), range(nz // 2, nz)
+    spread_near(1)
+    spread_far(1, far)
     for j in range(1, nt):
         logit_part(j).start()
-    pass_on(0, near)
-    spread(1)
 
     def item(i):
-        if i < 2:
-            h = zhalf if i == 0 else 1 - zhalf
-            return 0, pl.ds(pl.multiple_of(h * quarter, quarter), quarter)
-        return i - 1, pl.ds(0, half)
+        if i == 4:
+            return 2, pl.ds(0, half)
+        h = 1 - zhalf if i % 2 else zhalf
+        return i // 2, pl.ds(pl.multiple_of(h * quarter, quarter), quarter)
 
     def pair(i, c):
         a, span = item(i)
@@ -373,46 +442,64 @@
     def cols(c):
         return pl.ds(pl.multiple_of(c * fc, fc), fc)
 
-    def back_pass(i, start, stop):
-        _, span = item(i)
-        upper_span = pl.ds(pl.multiple_of(half + span.start, quarter), quarter)
-
+    def product(i, c):
+        if i == 4:
+            return jnp.dot(o_norm[...], wu[:, cols(c)], preferred_element_type=f32)
+        span = item(i)[1]
+        span_b = pl.ds(pl.multiple_of(half + span.start, quarter), quarter)
+        rows_of = gathered[i // 2]
+        left = jnp.concatenate([rows_of[span, :], rows_of[span_b, :]], axis=0)
+        if i < 2:
+            return nt_dot(left, wd[cols(c), :])
+        return jnp.dot(left, wg[:, cols(c)], preferred_element_type=f32)
+
+    def row_pass(i, start, stop, lag, before=()):
         @pl.loop(start, stop)
         def _(c):
-            left = jnp.concatenate([o_ups[span, :], o_ups[upper_span, :]], axis=0)
-            emit(i, c, nt_dot(left, wd[cols(c), :]))
-            if i == 1 and start == 0:
+            emit(i, c, product(i, c))
+            if before:
 
                 @pl.when(c == 0)
                 def _():
-                    relay(0, nc - 1)
-
-            @pl.when(c > 1)
+                    for b in before:
+                        relay(*b)
+
+            @pl.when(c >= lag)
             def _():
-                relay(i, c - 2)
+                relay(i, c - lag)
 
     cut, cut2 = nc // 3, 2 * nc // 3
+    far_a, far_b = far[: len(far) // 2], far[len(far) // 2 :]
     loads[0].wait()
-    arrived(0, [0, *near])
-    back_pass(0, 0, cut)
+    arrived_near(0)
+    row_pass(0, 0, cut, 2)
     share_logits()
-    pass_on(0, far)
-    back_pass(0, cut, cut2)
-    pass_on(1, near)
-    back_pass(0, cut2, nc)
+    row_pass(0, cut, cut2, 2)
+    pass_on(0, far_a)
+    row_pass(0, cut2, nc, 2)
     relay(0, nc - 2)
-    arrived(0, far)
-    back_pass(1, 0, cut)
-    pass_on(1, far)
-    back_pass(1, cut, nc)
+    pass_on(0, far_b)
+    loads[1].wait()
+    arrived_near(1)
+    row_pass(2, 0, cut2, 3, [(0, nc - 1)])
+    pass_on(1, far_a)
+    row_pass(2, cut2, nc, 3)
+    relay(2, nc - 3)
+    arrived_far(0)
+    results[4].start()
+    row_pass(1, 0, cut, 2, [(2, nc - 2), (2, nc - 1)])
+    pass_on(1, far_b)
+    row_pass(1, cut, nc, 2)
     relay(1, nc - 2)
-    arrived(1, range(nz))
-    loads[1].wait()
     loads[2].wait()
+    arrived_far(1)
+    results[3].start()
 
     @pl.loop(0, nc)
     def _(c):
-        emit(2, c, jnp.dot(o_norm[...], wg[:, cols(c)], preferred_element_type=f32))
+        values = [product(3, c), product(4, c)]
+        emit(3, c, values[0])
+        emit(4, c, values[1])
 
         @pl.when(c == 0)
         def _():
@@ -420,17 +507,11 @@
 
         @pl.when(c > 0)
         def _():
-            relay(2, c - 1)
-
-        emit(3, c, jnp.dot(o_norm[...], wu[:, cols(c)], preferred_element_type=f32))
-
-        @pl.when(c > 0)
-        def _():
             relay(3, c - 1)
-
-    relay(2, nc - 1)
+            relay(4, c - 1)
+
     relay(3, nc - 1)
-
+    relay(4, nc - 1)
     for j in range(1, ns):
         logit_copy(j).wait_recv()
     rgacc[...] = jnp.zeros_like(rgacc)
@@ -449,7 +530,7 @@
         return add
 
     def gate_backward(c):
-        for i in range(4):
+        for i in range(5):
             for j in range(1, nx):
                 cross(j, i, c).wait_recv()
 
@@ -496,19 +577,12 @@
         for a in range(3):
             act_copy(a, c).wait_recv()
 
-    na = nk // 2 if nk % 2 == 0 else nk
-    ka = width // na
-
-    def accumulate(c):
-        act_wait(c)
-
-        @pl.loop(0, na)
-        def _(k):
-            wide = pl.ds(pl.multiple_of(k * ka, ka), ka)
-            total = nt_dot(o_dg[:, cols(c)], wg[wide, cols(c)]) + nt_dot(
-                o_du[:, cols(c)], wu[wide, cols(c)]
-            )
-            acc[:, :, wide] = acc[:, :, wide] + total.reshape(ns, cap, ka)
+    def accumulate(c, start, stop):
+        wide = pl.ds(start, stop - start)
+        total = nt_dot(o_dg[:, cols(c)], wg[wide, cols(c)]) + nt_dot(
+            o_du[:, cols(c)], wu[wide, cols(c)]
+        )
+        acc[:, :, wide] = acc[:, :, wide] + total.reshape(ns, cap, stop - start)
 
     @pl.loop(0, nc - 1)
     def _(c):
@@ -516,9 +590,12 @@
 
         @pl.when(c > 0)
         def _():
-            accumulate(c - 1)
+            act_wait(c - 1)
+            accumulate(c - 1, 0, width // 2)
+            accumulate(c - 1, width // 2, width)
 
     gate_backward(nc - 1)
+    split = nk // 2
     rg_half = jnp.sum(rgacc[...], axis=1, keepdims=True)
     in_half = jnp.sum(inacc[...], axis=1, keepdims=True)
     in_half = in_half + rg_half * logbuf[pl.ds(mine, half), 0:1]
@@ -527,8 +604,11 @@
     rg_piece = rgbuf.at[pl.ds(mine, half), :]
     rg_copy = remote(rg_piece, rg_piece, rg_s, rg_r, tensor=mate)
     rg_copy.start()
-    accumulate(nc - 2)
+    act_wait(nc - 2)
+    accumulate(nc - 2, 0, split * kc)
     act_wait(nc - 1)
+    for a in range(3):
+        results[a].start()
     rg_copy.wait_recv()
 
     def ycopy(k):
@@ -557,80 +637,123 @@
         acc[:, :, kcols(k)] = total
         for zz in range(nz):
             ysnd[k, zz] = acc[(1 - y) * nz + zz, :, kcols(k)].astype(bf16)
-        gsnd[0:1, kcols(k)] = jnp.sum(
+        bsnd[:, kcols(k)] = jnp.sum(
             total.reshape(rows, kc) * o_norm[:, kcols(k)].astype(f32), axis=0, keepdims=True
         ) / gain[:, kcols(k)]
 
-    @pl.loop(0, nk - 1)
-    def _(k):
-        finish(k)
-        ycopy(k).start()
-
-    extra = gsnd.shape[1] - width
-    gsnd[0:1, pl.ds(width, extra)] = rgbuf[...].T[64:65, :]
-    gsnd[1:2, pl.ds(width, extra)] = jnp.broadcast_to(live[...].astype(f32), (1, extra))
+    def sum_y(i):
+        return remote(sums[i][0], sums[i][1], gy_s.at[i], gy_r.at[i], seq=yp)
+
+    def sum_z(i, j):
+        return remote(
+            sums[i][2], sums[i][3].at[j], gz_s.at[i, j], gz_r.at[i, j], seq=2 * zx(j) + y
+        )
+
+    def sum_middle(i):
+        sum_y(i).wait_recv()
+        sums[i][2][...] = sums[i][0][...] + sums[i][1][...]
+        for j in range(1, nz):
+            sum_z(i, j).start()
+
+    def sum_end(i):
+        total = sums[i][2][...]
+        for j in range(1, nz):
+            sum_z(i, j).wait_recv()
+            total = total + sums[i][3][j]
+        return total
+
+    sums = ((asnd, ayrec, azsnd, azrec), (bsnd, byrec, bzsnd, bzrec))
+    finish(0)
+    ycopy(0).start()
     router_part = jnp.zeros((1, width), f32)
     for b in range(ns):
         block = o_norm[b * cap : (b + 1) * cap, :].astype(f32)
         router_part = router_part + jnp.sum(
             rgbuf[b * cap : (b + 1) * cap, 0:1] * block, axis=0, keepdims=True
         )
-    gsnd[1:2, pl.ds(0, width)] = router_part
-    finish(nk - 1)
-    gy_copy = remote(gsnd, gyrec, gy_s, gy_r, seq=yp)
-    gy_copy.start()
-    ycopy(nk - 1).start()
-
-    def gz_copy(j):
-        return remote(gzsnd, gzrec.at[j], gz_s.at[j], gz_r.at[j], seq=2 * zx(j) + y)
-
-    @pl.loop(0, nk - 1)
+    asnd[:, pl.ds(0, width)] = router_part
+    asnd[:, pl.ds(width, rows)] = rgbuf[...].T[64:65, :]
+    asnd[:, pl.ds(width + rows, 128)] = jnp.broadcast_to(live[...].astype(f32), (1, 128))
+    sum_y(0).start()
+    held = max(nk - 2, 1)
+
+    @pl.loop(1, split)
+    def _(k):
+        finish(k)
+        ycopy(k).start()
+
+    accumulate(nc - 2, split * kc, width)
+
+    @pl.loop(split, held)
+    def _(k):
+        finish(k)
+        ycopy(k).start()
+
+    for k in range(held, nk):
+        finish(k)
+    sum_y(1).start()
+    for k in range(held, nk):
+        ycopy(k).start()
+    zstage(0)
+    sum_middle(0)
+
+    @pl.loop(1, held)
     def _(k):
         zstage(k)
 
-    gy_copy.wait_recv()
-    gzsnd[...] = gsnd[...] + gyrec[...]
-    for j in range(1, nz):
-        gz_copy(j).start()
-    zstage(nk - 1)
-
-    o_dn[...] = acc[y * nz + z]
-    for j in range(1, nz):
-
-        @pl.loop(0, nk)
-        def _(k):
+    sum_middle(1)
+    for k in range(held, nk):
+        zstage(k)
+    total = sum_end(0)
+    scale = lax.rsqrt(total[:, width + rows :])
+    o_cs[...] = scale
+    results[5].start()
+    o_fin[cap : cap + 8, :] = jnp.zeros((8, width), f32)
+    o_fin[cap + 1 : cap + 2, :] = total[:, 0:width] * scale[:, 0:1]
+    here = (y * nz + z) * cap + lax.broadcasted_iota(jnp.int32, (cap, rows), 0)
+    pick = here == lax.broadcasted_iota(jnp.int32, (cap, rows), 1)
+    inner = jnp.sum(
+        jnp.where(pick, total[:, width : width + rows], 0.0), axis=1, keepdims=True
+    )
+    inner = inner / width_total
+    inverse = invbuf[:, 0:1]
+    alive = (lax.broadcasted_iota(jnp.int32, (cap, 1), 0) < live[...]).astype(f32)
+    o_fin[cap : cap + 1, :] = sum_end(1) * scale[:, 0:1]
+
+    @pl.loop(0, nk)
+    def _(k):
+        d_normed = acc[y * nz + z, :, kcols(k)]
+        for j in range(1, nz):
             zcopy(j, k).wait_recv()
-            o_dn[:, kcols(k)] = o_dn[:, kcols(k)] + zrec[j, k].astype(f32)
-
-    total = gzsnd[...]
-    for j in range(1, nz):
-        gz_copy(j).wait_recv()
-        total = total + gzrec[j]
-    o_gr[...] = total[:, 0:width]
-    o_cs[...] = lax.rsqrt(total[1:2, width : width + 128])
-    here = (y * nz + z) * cap + lax.broadcasted_iota(jnp.int32, (cap, extra), 0)
-    pick = here == lax.broadcasted_iota(jnp.int32, (cap, extra), 1)
-    inner = jnp.sum(jnp.where(pick, total[0:1, width:], 0.0), axis=1, keepdims=True)
-    o_col[1] = jnp.broadcast_to(inner / width_total, (cap, 128))
-
+            d_normed = d_normed + zrec[j, k].astype(f32)
+        scaled = own[:, kcols(k)] * inverse
+        o_fin[0:cap, kcols(k)] = (
+            inverse * (d_normed * gain[:, kcols(k)] - scaled * inner) * alive
+        )
+
+    results[6].start()
     for m in range(2):
-        agy(m, 0).wait_send()
-        for j in range(1, nz):
+        agy_own(m).wait_send()
+        for j in near:
             agz(m, j).wait_send()
+            agd(m, j).wait_send()
+        for j in far:
+            agf(m, j).wait_send()
             agy(m, j).wait_send()
     for j in range(1, nt):
         square_copy(j).wait_send()
         logit_part(j).wait_send()
     for j in range(1, ns):
         logit_copy(j).wait_send()
-    gy_copy.wait_send()
-    for j in range(1, nz):
-        gz_copy(j).wait_send()
+    for i in range(2):
+        sum_y(i).wait_send()
+        for j in range(1, nz):
+            sum_z(i, j).wait_send()
     rg_copy.wait_send()
 
     @pl.loop(0, nc)
     def _(c):
-        for i in range(4):
+        for i in range(5):
             pair(i, c).wait_send()
             for j in range(1, nx):
                 cross(j, i, c).wait_send()
@@ -642,6 +765,9 @@
         ycopy(k).wait_send()
         for j in range(1, nz):
             zcopy(j, k).wait_send()
+
+    for result in results:
+        result.wait()
 
 
 def body(
@@ -662,16 +788,16 @@
     rows, nz, nx = ns * cap, ns // 2, nt // 2
     half = rows // 2
     nc = pick_chunks(hidden, (6, 4, 3, 2))
-    nk = pick_chunks(width, (4, 2))
+    nk = pick_chunks(width, (8, 4, 2))
     fc, kc = hidden // nc, width // nk
-    wide = width + rows
+    wide = width + rows + 128
     vmem = pl.BlockSpec(memory_space=pltpu.VMEM)
     hbm = pl.BlockSpec(memory_space=pl.ANY)
     dma = pltpu.SemaphoreType.DMA
     tok = slot_tokens.reshape(1, cap)
     live = live_counts.reshape(1, 1)
     gain = norm_gain.reshape(1, width)
-    weighted, d_gate, d_up, normed, upstream, sums, scale, d_normed, column = pl.pallas_call(
+    weighted, d_gate, d_up, normed, upstream, scale, final = pl.pallas_call(
         functools.partial(kernel, ns, nt, nc, nk),
         out_shape=[
             jax.ShapeDtypeStruct((rows, hidden), bf16),
@@ -679,18 +805,24 @@
             jax.ShapeDtypeStruct((rows, hidden), bf16),
             jax.ShapeDtypeStruct((rows, width), bf16),
             jax.ShapeDtypeStruct((rows, width), bf16),
-            jax.ShapeDtypeStruct((2, width), f32),
             jax.ShapeDtypeStruct((1, 128), f32),
-            jax.ShapeDtypeStruct((cap, width), f32),
-            jax.ShapeDtypeStruct((2, cap, 128), f32),
+            jax.ShapeDtypeStruct((cap + 8, width), f32),
         ],
         in_specs=[vmem] * 6 + [hbm] * 3,
-        out_specs=[vmem] * 9,
+        out_specs=[hbm] * 7,
         scratch_shapes=[
+            pltpu.VMEM((rows, hidden), bf16),
+            pltpu.VMEM((rows, hidden), bf16),
+            pltpu.VMEM((rows, hidden), bf16),
+            pltpu.VMEM((rows, width), bf16),
+            pltpu.VMEM((rows, width), bf16),
+            pltpu.VMEM((1, 128), f32),
+            pltpu.VMEM((cap + 8, width), f32),
             pltpu.VMEM((width, hidden), bf16),
             pltpu.VMEM((width, hidden), bf16),
             pltpu.VMEM((hidden, width), bf16),
             pltpu.VMEM((cap, width), f32),
+            pltpu.VMEM((cap, 128), f32),
             pltpu.VMEM((cap, 128), f32),
             pltpu.VMEM((nt, cap, 128), f32),
             pltpu.VMEM((cap, 128), f32),
@@ -708,11 +840,18 @@
             pltpu.VMEM((nk, nz, cap, kc), bf16),
             pltpu.VMEM((nz, nk, cap, kc), bf16),
             pltpu.VMEM((nz, nk, cap, kc), bf16),
-            pltpu.VMEM((2, wide), f32),
-            pltpu.VMEM((2, wide), f32),
-            pltpu.VMEM((2, wide), f32),
-            pltpu.VMEM((nz, 2, wide), f32),
+            pltpu.VMEM((1, wide), f32),
+            pltpu.VMEM((1, wide), f32),
+            pltpu.VMEM((1, wide), f32),
+            pltpu.VMEM((nz, 1, wide), f32),
+            pltpu.VMEM((1, width), f32),
+            pltpu.VMEM((1, width), f32),
+            pltpu.VMEM((1, width), f32),
+            pltpu.VMEM((nz, 1, width), f32),
             dma((3,)),
+            dma((7,)),
+            dma((2, nz)),
+            dma((2, nz)),
             dma((2, nz)),
             dma((2, nz)),
             dma((2, nz)),
@@ -723,10 +862,10 @@
             dma((nt,)),
             dma((ns,)),
             dma((ns,)),
-            dma((4, nc)),
-            dma((4, nc)),
-            dma((nx, 4, nc)),
-            dma((nx, 4, nc)),
+            dma((5, nc)),
+            dma((5, nc)),
+            dma((nx, 5, nc)),
+            dma((nx, 5, nc)),
             dma((3, nc)),
             dma((3, nc)),
             dma,
@@ -735,10 +874,10 @@
             dma((nk,)),
             dma((nz, nk)),
             dma((nz, nk)),
-            dma,
-            dma,
-            dma((nz,)),
-            dma((nz,)),
+            dma((2,)),
+            dma((2,)),
+            dma((2, nz)),
+            dma((2, nz)),
         ],
         compiler_params=pltpu.CompilerParams(
             collective_id=0, has_side_effects=True, vmem_limit_bytes=67_043_328
@@ -760,15 +899,10 @@
         d_up,
         weighted,
         upstream,
-        hidden_in,
+        scale,
+        tok,
         grad_out,
-        d_normed,
-        gain,
-        sums,
-        scale,
-        column,
-        tok,
-        live,
+        final,
     )
     return (
         grad_in,

time: 84.3 us -> 81.5 us (0.967)
  Pallas kernels: 82.8 us -> 80 us
    pallas_call x1, Pallas kernels: 66.5 us -> 63.9 us  [body(): pl.pallas_call(functools.partial(kernel, ns, nt, nc, nk), out_shape=[jax....]
where the time goes in v2:
time: 81.5 us; the launch traced here: 81.3 us
  Pallas kernels  80 us (98%)
  between operations  1.29 us (2%)
    pallas_call x1, Pallas kernels, body(): pl.pallas_call(functools.partial(kernel, ns, nt, nc, nk), out_shape=[jax....  63.9 us
    pallas_call x1, Pallas kernels, outer_products(): pl.pallas_call(outer_kernel, grid=(steps,), out_shape=[jax.ShapeDtypeStru...  16.1 us

profile of v2, /device:TPU:0, one launch (start us, length us, event | category | flops | bytes accessed | tf_op | source)
XLA Modules:
  0.0 81.3 jit_solution(10610803498846299169)
XLA Ops:
  1.3 63.9 %shard_map.136 = (bf16[128,3072]{1,0:T(8,128)(2,1)}, bf16[128,3072]{1,0:T(8,128)(2,1)}, bf16[128,3072]{1,0:T(8,128)(2,1)}, bf16[128,2048]{1,0:T(8,128)(2,1)}, bf...) custom-call(bf16[128,2048]{1,0:T(8,128)(2,1)} %hid.1, bf16[128,2048]{1,0:T(8,128)(2,1)} %gout_hbm.1, ...), custom_call_target="tpu_custom_call" | custom-call | tf_op jit(solution)/shard_map/pallas_call | solution.py:800
  65.2 16.1 %shard_map.137 = (bf16[2048,3072]{1,0:T(8,128)(2,1)}, bf16[2048,3072]{1,0:T(8,128)(2,1)}, bf16[3072,2048]{1,0:T(8,128)(2,1)}, bf16[128,2048]{1,0:T(8,128)(2,1)}, f32[1,2048]{1,0:T(1,128)}, /*index=5*/f32[1,2048]{1,0:T(1,128)}) custom-call(bf16[128,2048]{1,0:T(8,128)(2,1)} %get-tuple-element.19.norm, bf16[128,3072]{1,0:T(8,128)(2,1)} %get-tuple-element.20.dg, ...), custom_call_target="tpu_custom_call" | custom-call | tf_op jit(solution)/shard_map/pallas_call | solution.py:89

commit v3 on v2

--- a/solution.py
+++ b/solution.py
@@ -418,8 +418,8 @@
         return remote(
             xsnd.at[a, c, span],
             xrec.at[j, a, c, span],
-            x_s.at[j, i, c],
-            x_r.at[j, i, c],
+            x_s.at[j - 1, i, c],
+            x_r.at[j - 1, i, c],
             tensor=2 * lax.rem(x + j, nx) + core,
         )
 
@@ -618,8 +618,8 @@
         return remote(
             zsnd.at[j, k],
             zrec.at[j, k],
-            z_s.at[j, k],
-            z_r.at[j, k],
+            z_s.at[j - 1, k],
+            z_r.at[j - 1, k],
             seq=2 * zx(j) + y,
         )
 
@@ -864,16 +864,16 @@
             dma((ns,)),
             dma((5, nc)),
             dma((5, nc)),
-            dma((nx, 5, nc)),
-            dma((nx, 5, nc)),
+            dma((nx - 1, 5, nc)),
+            dma((nx - 1, 5, nc)),
             dma((3, nc)),
             dma((3, nc)),
             dma,
             dma,
             dma((nk,)),
             dma((nk,)),
-            dma((nz, nk)),
-            dma((nz, nk)),
+            dma((nz - 1, nk)),
+            dma((nz - 1, nk)),
             dma((2,)),
             dma((2,)),
             dma((2, nz)),

time: 81.5 us -> 80.8 us (level)
  no operation moved by 1% of the time
where the time goes in v3:
time: 80.8 us; the launch traced here: 80.7 us
  Pallas kernels  79.4 us (98%)
  between operations  1.29 us (2%)
    pallas_call x1, Pallas kernels, body(): pl.pallas_call(functools.partial(kernel, ns, nt, nc, nk), out_shape=[jax....  63.3 us
    pallas_call x1, Pallas kernels, outer_products(): pl.pallas_call(outer_kernel, grid=(steps,), out_shape=[jax.ShapeDtypeStru...  16.1 us

profile of v3, /device:TPU:0, one launch (start us, length us, event | category | flops | bytes accessed | tf_op | source)
XLA Modules:
  0.0 80.7 jit_solution(16524309417202025517)
XLA Ops:
  1.3 63.3 %shard_map.136 = (bf16[128,3072]{1,0:T(8,128)(2,1)}, bf16[128,3072]{1,0:T(8,128)(2,1)}, bf16[128,3072]{1,0:T(8,128)(2,1)}, bf16[128,2048]{1,0:T(8,128)(2,1)}, bf...) custom-call(bf16[128,2048]{1,0:T(8,128)(2,1)} %hid.1, bf16[128,2048]{1,0:T(8,128)(2,1)} %gout_hbm.1, ...), custom_call_target="tpu_custom_call" | custom-call | tf_op jit(solution)/shard_map/pallas_call | solution.py:800
  64.5 16.1 %shard_map.137 = (bf16[2048,3072]{1,0:T(8,128)(2,1)}, bf16[2048,3072]{1,0:T(8,128)(2,1)}, bf16[3072,2048]{1,0:T(8,128)(2,1)}, bf16[128,2048]{1,0:T(8,128)(2,1)}, f32[1,2048]{1,0:T(1,128)}, /*index=5*/f32[1,2048]{1,0:T(1,128)}) custom-call(bf16[128,2048]{1,0:T(8,128)(2,1)} %get-tuple-element.19.norm, bf16[128,3072]{1,0:T(8,128)(2,1)} %get-tuple-element.20.dg, ...), custom_call_target="tpu_custom_call" | custom-call | tf_op jit(solution)/shard_map/pallas_call | solution.py:89
